TPU v7x, 64 devices: a 2x2x8 block of a 4x4x8 slice. The times are simulated.
64 devices in a mesh: rep: 8 (over x, y, core), dp: 8 (over z).
Axes of the slice: x: 2, y: 2, z: 8, core: 2. Of those that a mesh axis runs over, the one named last changes fastest.
The devices are a block of a 4x4x8 slice.
Arguments:
- x: bfloat16 [64, 2048, 512], P(('rep', 'dp')), parts along dimension 0
- dy: bfloat16 [64, 2048, 512], P(('rep', 'dp')), parts along dimension 0
- w_gate: bfloat16 [2, 512, 2048], P(None, 'dp')
- w_up: bfloat16 [2, 512, 2048], P(None, 'dp')
- w_down: bfloat16 [2, 2048, 512], P(None, 'dp')
- m_w_gate: float32 [2, 512, 2048], P(None, 'dp')
- m_w_up: float32 [2, 512, 2048], P(None, 'dp')
- m_w_down: float32 [2, 2048, 512], P(None, 'dp')
- v_w_gate: float32 [2, 512, 2048], P(None, 'dp')
- v_w_up: float32 [2, 512, 2048], P(None, 'dp')
- v_w_down: float32 [2, 2048, 512], P(None, 'dp')
Outputs:
- output 1: bfloat16 [16, 512, 2048], P('rep', 'dp'), parts along dimension 0
- output 2: bfloat16 [16, 512, 2048], P('rep', 'dp'), parts along dimension 0
- output 3: bfloat16 [16, 2048, 512], P('rep', 'dp'), parts along dimension 0
- output 4: float32 [16, 512, 2048], P('rep', 'dp'), parts along dimension 0
- output 5: float32 [16, 512, 2048], P('rep', 'dp'), parts along dimension 0
- output 6: float32 [16, 2048, 512], P('rep', 'dp'), parts along dimension 0
- output 7: float32 [16, 512, 2048], P('rep', 'dp'), parts along dimension 0
- output 8: float32 [16, 512, 2048], P('rep', 'dp'), parts along dimension 0
- output 9: float32 [16, 2048, 512], P('rep', 'dp'), parts along dimension 0
There are 8 independent parts. A program takes and returns all parts, laid end to end along the dimension named above; an argument that names none is the same for every part.
All inputs are finite; a program needn't handle non-finite values.
Results may differ from a plain program's by a relative error of at most 0.022.
Values are sent between devices in bfloat16 or wider.
A program may use at most 768 MiB of HBM per device.

v0:
```python
import jax
import jax.numpy as jnp
from jax import lax
from jax.sharding import PartitionSpec as P

NAMES = ("w_gate", "w_up", "w_down")


def matmul(a, w):
    return jnp.dot(a, w, preferred_element_type=jnp.float32).astype(jnp.bfloat16)


def normed(h):
    wide = h.astype(jnp.float32)
    scale = lax.rsqrt(jnp.mean(wide**2, -1, keepdims=True) + 1e-6)
    return (wide * scale).astype(jnp.bfloat16)


def layer(h, w):
    a = normed(h)
    gate = jnp.dot(a, w["w_gate"], preferred_element_type=jnp.float32)
    up = jnp.dot(a, w["w_up"], preferred_element_type=jnp.float32)
    return h + matmul((jax.nn.silu(gate) * up).astype(jnp.bfloat16), w["w_down"])


def adamw(w, m, v, g):
    m = 0.9 * m + 0.1 * g
    v = 0.95 * v + 0.05 * g * g
    step = m * lax.rsqrt(v + 1e-8) + 0.1 * w
    return (w - 0.02 * step).astype(jnp.bfloat16), m, v


def clipped(gradients, sum_of_squares, count):
    factor = jnp.minimum(1.0, 0.5 * lax.rsqrt(sum_of_squares / count + 1e-30))
    return [g * factor for g in gradients]


def solution(mesh):
    def fetched(weights, number):
        return {name: lax.all_gather(w[number], "dp", axis=0, tiled=True) for name, w in zip(NAMES, weights, strict=True)}

    def step(x, dy, *arrays):
        weights, m, v = (arrays[i : i + 3] for i in (0, 3, 6))
        layers = weights[0].shape[0]
        h, kept = x[0], []
        for number in range(layers):
            kept.append(h)
            h = layer(h, fetched(weights, number))
        by_h, mine = dy[0], [None] * layers
        for number in reversed(range(layers)):
            _, back = jax.vjp(lambda w, h: layer(h, w), fetched(weights, number), kept[number])
            by_w, by_h = back(by_h)
            mine[number] = [lax.psum_scatter(by_w[name], "dp", scatter_dimension=0, tiled=True) for name in NAMES]
        gradients = [jnp.stack([mine[number][i] for number in range(layers)]).astype(jnp.float32) for i in range(3)]
        squares = lax.psum(sum(jnp.sum(g * g) for g in gradients), "dp")
        gradients = clipped(gradients, squares, lax.psum(1, "dp") * sum(g.size for g in gradients))
        new = [adamw(w.astype(jnp.float32), m, v, g) for w, m, v, g in zip(weights, m, v, gradients, strict=True)]
        return tuple(one[which] for which in range(3) for one in new)

    states, cut = P(("rep", "dp"), None, None), P(None, "dp", None)
    return jax.shard_map(
        step,
        mesh=mesh,
        in_specs=(states, states) + (cut,) * 9,
        out_specs=(P("rep", "dp", None),) * 9,
        check_vma=False,
    )
```

profile of v0, /device:TPU:22, one launch (start us, length us, event | category | flops | bytes accessed | tf_op | source)
XLA Modules:
  0.0 565.1 jit_solution(4014193388102337620)
XLA Ops:
  15.2 2.9 copy.20
  18.6 4.2 copy.21
  22.8 28.8 %all-gather.13.cloned.1.call-done = bf16[1,512,2048]{2,1,0:T(8,128)(2,1)} async-done(((bf16[1,64,2048]{2,1,0:T(8,128)(2,1)}), bf16[1,512,2048]{2,1,0:T(8,128)(2,1)}) %all-gather.13.cloned.1.call-update) | async-done | bytes 2097168 | tf_op jit(solution)/shard_map/all_gather | solution.py:40
  51.5 9.7 %fusion.46 = f32[2048,2048]{1,0:T(8,128)} fusion(bf16[1,512,2048]{2,1,0:T(8,128)(2,1)} %all-gather.13.cloned.1.call-done, bf16[1,2048,512]{1,2,0:T(8,128)(2,1)S(1)} %copy.20, f32[2048]{0:T(1024)S(1)} %add_rsqrt_fusion), kind=kOutput, calls=%fused_computation.65 | convolution fusion | flops 4298113024 | bytes 20979712 | tf_op jit(solution)/shard_map/dot_general | solution.py:21
  61.2 28.3 %all-gather.15.cloned.1.call-done = bf16[1,512,2048]{2,1,0:T(8,128)(2,1)} async-done(((bf16[1,64,2048]{2,1,0:T(8,128)(2,1)}), bf16[1,512,2048]{2,1,0:T(8,128)(2,1)}) %all-gather.15.cloned.1.call-update) | async-done | bytes 2097168 | tf_op jit(solution)/shard_map/all_gather | solution.py:40
  89.6 16.2 %multiply_convert_fusion.1 = (bf16[2048,2048]{1,0:T(8,128)(2,1)}, f32[2048,2048]{1,0:T(8,128)}) fusion(f32[2048,2048]{1,0:T(8,128)} %fusion.46, bf16[1,512,2048]{2,1,0:T(8,128)(2,1)} %all-gather.15.cloned.1.call-done, bf16[1,2048,512]{1,2,0:T(8,128)(2,1)S(1)} %copy.20, f32[2048]{0:T(1024)S(1)} %add_rsqrt_fusion), kind=kOutput, calls=%fused_computation.17 | convolution fusion | flops 4323278848 | bytes 46145536 | tf_op jit(solution)/shard_map/dot_general | solution.py:22
  105.8 21.8 %all-gather.17.cloned.1.call-done = bf16[1,2048,512]{2,1,0:T(8,128)(2,1)} async-done(((bf16[1,256,512]{2,1,0:T(8,128)(2,1)}), bf16[1,2048,512]{2,1,0:T(8,128)(2,1)}) %all-gather.17.cloned.1.call-update) | async-done | bytes 2097168 | tf_op jit(solution)/shard_map/all_gather | solution.py:40
  127.6 10.2 %fusion.19 = (f32[2048]{0:T(1024)S(1)}, bf16[2048,512]{0,1:T(8,128)(2,1)}) fusion(bf16[2048,2048]{1,0:T(8,128)(2,1)} %get-tuple-element.24, bf16[1,2048,512]{2,1,0:T(8,128)(2,1)} %all-gather.17.cloned.1.call-done, bf16[1,2048,512]{1,2,0:T(8,128)(2,1)S(1)} %copy.20), kind=kOutput, calls=%fused_computation.37 | convolution fusion | flops 4300208128 | bytes 14688256 | tf_op jit(solution)/shard_map/dot_general | solution.py:10
  137.8 27.7 %all-gather.21.cloned.1.call-done = bf16[1,2048,512]{2,1,0:T(8,128)(2,1)} async-done(((bf16[1,256,512]{2,1,0:T(8,128)(2,1)}), bf16[1,2048,512]{2,1,0:T(8,128)(2,1)}) %all-gather.21.cloned.1.call-update) | async-done | bytes 2097168 | tf_op jit(solution)/shard_map/all_gather | solution.py:40
  165.4 10.1 %convolution_convert_fusion.1 = bf16[2048,2048]{1,0:T(8,128)(2,1)} fusion(bf16[1,2048,512]{2,1,0:T(8,128)(2,1)} %param.12, bf16[1,2048,512]{2,1,0:T(8,128)(2,1)} %all-gather.21.cloned.1.call-done), kind=kOutput, calls=%fused_computation.25 | convolution fusion | flops 4299161600 | bytes 12582912 | tf_op jit(solution)/shard_map/transpose(jvp())/dot_general | solution.py:10
  175.5 27.8 %all-gather.23.cloned.1.call-done = bf16[1,512,2048]{2,1,0:T(8,128)(2,1)} async-done(((bf16[1,64,2048]{2,1,0:T(8,128)(2,1)}), bf16[1,512,2048]{2,1,0:T(8,128)(2,1)}) %all-gather.23.cloned.1.call-update) | async-done | bytes 2097168 | tf_op jit(solution)/shard_map/all_gather | solution.py:40
  203.3 9.7 %fusion.35 = f32[2048,2048]{1,0:T(8,128)} fusion(bf16[1,512,2048]{2,1,0:T(8,128)(2,1)} %all-gather.23.cloned.1.call-done, bf16[2048,512]{0,1:T(8,128)(2,1)S(1)} %copy-done.7, f32[2048]{0:T(1024)S(1)} %fusion.77), kind=kOutput, calls=%fused_computation.54 | convolution fusion | flops 4298113024 | bytes 20979712 | tf_op jit(solution)/shard_map/jvp()/dot_general | solution.py:22
  213.0 28.2 %all-gather.19.cloned.1.call-done = bf16[1,512,2048]{2,1,0:T(8,128)(2,1)} async-done(((bf16[1,64,2048]{2,1,0:T(8,128)(2,1)}), bf16[1,512,2048]{2,1,0:T(8,128)(2,1)}) %all-gather.19.cloned.1.call-update) | async-done | bytes 2097168 | tf_op jit(solution)/shard_map/all_gather | solution.py:40
  241.2 21.1 %fusion.2 = (bf16[2048,2048]{1,0:T(8,128)(2,1)}, f32[2048,2048]{1,0:T(8,128)}) fusion(f32[2048,2048]{1,0:T(8,128)} %fusion.35, bf16[2048,2048]{1,0:T(8,128)(2,1)} %convolution_convert_fusion.1, bf16[1,512,2048]{2,1,0:T(8,128)(2,1)} %all-gather.19.cloned.1.call-done, bf16[2048,512]{0,1:T(8,128)(2,1)S(1)} %copy-done.7, f32[2048]{0:T(1024)S(1)} %fusion.77), kind=kOutput, calls=%fused_computation.8 | convolution fusion | flops 4348444672 | bytes 54534144 | tf_op jit(solution)/shard_map/jvp()/dot_general | solution.py:21
  262.2 11.7 %fusion.26 = bf16[2048,512]{0,1:T(8,128)(2,1)S(1)} fusion(bf16[2048,2048]{1,0:T(8,128)(2,1)} %convolution_convert_fusion.1, bf16[1,512,2048]{2,1,0:T(8,128)(2,1)} %all-gather.23.cloned.1.call-done, f32[2048,2048]{1,0:T(8,128)} %get-tuple-element.29), kind=kOutput, calls=%fused_computation.44 | convolution fusion | flops 4321181696 | bytes 29360128 | tf_op jit(solution)/shard_map/transpose(jvp())/dot_general | solution.py:22
  274.1 5.0 fusion.21
  281.9 9.8 %convolution_convert_fusion.2 = bf16[2048,512]{1,0:T(8,128)(2,1)} fusion(bf16[2048,2048]{1,0:T(8,128)(2,1)} %get-tuple-element.24, bf16[2048,512]{0,1:T(8,128)(2,1)S(1)} %fusion.32), kind=kOutput, calls=%fused_computation.42 | convolution fusion | flops 4296015872 | bytes 12582912 | tf_op jit(solution)/shard_map/transpose(jvp())/dot_general | solution.py:10
  291.8 14.5 %fusion.22 = bf16[2048,512]{1,0:T(8,128)(2,1)} fusion(f32[2048,2048]{1,0:T(8,128)} %fusion.35, bf16[1,2048,512]{2,1,0:T(8,128)(2,1)S(1)} %copy-done.6, f32[2048,2048]{1,0:T(8,128)} %get-tuple-element.29), kind=kOutput, calls=%fused_computation.40 | convolution fusion | flops 4321181696 | bytes 37748736 | tf_op jit(solution)/shard_map/transpose(jvp())/dot_general | solution.py:10
  306.5 6.9 %convolution_convert_fusion = bf16[2048,2048]{1,0:T(8,128)(2,1)S(1)} fusion(bf16[2048,512]{0,1:T(8,128)(2,1)} %copy-done.8, bf16[1,2048,512]{2,1,0:T(8,128)(2,1)} %all-gather.17.cloned.1.call-done), kind=kOutput, calls=%fused_computation.24 | convolution fusion | flops 4299161600 | bytes 12582912 | tf_op jit(solution)/shard_map/transpose(jvp())/dot_general | solution.py:10
  313.4 3.3 copy-done.20
  316.7 10.6 %fusion.28 = bf16[512,2048]{1,0:T(8,128)(2,1)} fusion(bf16[2048,2048]{1,0:T(8,128)(2,1)S(1)} %convolution_convert_fusion, f32[2048,2048]{1,0:T(8,128)} %fusion.46, bf16[1,2048,512]{1,2,0:T(8,128)(2,1)S(1)} %copy-done.1, f32[2048]{0:T(1024)S(1)} %copy-done.18), kind=kOutput, calls=%fused_computation.46 | convolution fusion | flops 4324327424 | bytes 29368320 | tf_op jit(solution)/shard_map/transpose(jvp())/dot_general | solution.py:22
  327.4 13.1 %fusion.27 = bf16[512,2048]{1,0:T(8,128)(2,1)} fusion(bf16[2048,2048]{1,0:T(8,128)(2,1)} %convolution_convert_fusion.1, bf16[2048,512]{0,1:T(8,128)(2,1)} %get-tuple-element.27, f32[2048]{0:T(1024)S(1)} %fusion.77, f32[2048,2048]{1,0:T(8,128)} %get-tuple-element.29), kind=kOutput, calls=%fused_computation.45 | convolution fusion | flops 4324327424 | bytes 29368320 | tf_op jit(solution)/shard_map/transpose(jvp())/dot_general | solution.py:22
  340.6 17.6 %fusion.23 = bf16[512,2048]{1,0:T(8,128)(2,1)} fusion(f32[2048,2048]{1,0:T(8,128)} %fusion.46, f32[2048,2048]{1,0:T(8,128)} %get-tuple-element.25, bf16[2048,2048]{1,0:T(8,128)(2,1)} %copy-done.20, bf16[1,2048,512]{1,2,0:T(8,128)(2,1)S(1)} %copy-done.1, f32[2048]{0:T(1024)S(1)} %copy-done.18), kind=kOutput, calls=%fused_computation.41 | convolution fusion | flops 4345298944 | bytes 46145536 | tf_op jit(solution)/shard_map/transpose(jvp())/dot_general | solution.py:21
  358.4 9.9 %convolution_convert_fusion.4 = bf16[512,2048]{1,0:T(8,128)(2,1)} fusion(bf16[2048,2048]{1,0:T(8,128)(2,1)} %get-tuple-element.28, bf16[2048,512]{0,1:T(8,128)(2,1)} %get-tuple-element.27, f32[2048]{0:T(1024)S(1)} %fusion.77), kind=kOutput, calls=%fused_computation.47 | convolution fusion | flops 4298113024 | bytes 12591104 | tf_op jit(solution)/shard_map/transpose(jvp())/dot_general | solution.py:21
  371.6 38.3 %reduce-scatter.11.cloned.1.call-done = bf16[64,2048]{1,0:T(8,128)(2,1)} async-done(((bf16[512,2048]{1,0:T(8,128)(2,1)}), bf16[64,2048]{1,0:T(8,128)(2,1)}) %reduce-scatter.11.cloned.1.call-update) | async-done | bytes 262160 | tf_op jit(solution)/shard_map/reduce_scatter | solution.py:53
  409.9 39.8 %reduce-scatter.13.cloned.1.call-done = bf16[64,2048]{1,0:T(8,128)(2,1)} async-done(((bf16[512,2048]{1,0:T(8,128)(2,1)}), bf16[64,2048]{1,0:T(8,128)(2,1)}) %reduce-scatter.13.cloned.1.call-update) | async-done | bytes 262160 | tf_op jit(solution)/shard_map/reduce_scatter | solution.py:53
  449.7 1.9 fusion.66
  451.7 38.5 %reduce-scatter.7.cloned.1.call-done = bf16[64,2048]{1,0:T(8,128)(2,1)} async-done(((bf16[512,2048]{1,0:T(8,128)(2,1)}), bf16[64,2048]{1,0:T(8,128)(2,1)}) %reduce-scatter.7.cloned.1.call-update) | async-done | bytes 262160 | tf_op jit(solution)/shard_map/reduce_scatter | solution.py:53
  490.2 40.1 %reduce-scatter.9.cloned.1.call-done = bf16[64,2048]{1,0:T(8,128)(2,1)} async-done(((bf16[512,2048]{1,0:T(8,128)(2,1)}), bf16[64,2048]{1,0:T(8,128)(2,1)}) %reduce-scatter.9.cloned.1.call-update) | async-done | bytes 262160 | tf_op jit(solution)/shard_map/reduce_scatter | solution.py:53
  534.1 16.1 %psum.7 = f32[]{:T(128)} all-reduce(f32[]{:T(128)S(6)} %add.99), channel_id=1, replica_groups=mesh['rep'=8,'dp'=8] {'dp'}, use_global_device_ids=true, to_apply=%region_12.13 | all-reduce | flops 1 | bytes 8 | tf_op jit(solution)/shard_map/psum | solution.py:55
  551.0 3.7 fusion.73
  554.8 3.0 fusion.64
  (79 shorter events, 16.9 us)
Async XLA Ops:
  7.2 44.4 %all-gather.13.cloned.1.call-start = ((), (), s32[]{:S(2)}) async-start(), calls=%async_computation.12 | async-start | bytes 2359296 | tf_op jit(solution)/shard_map/all_gather | solution.py:40
  9.2 80.4 %all-gather.15.cloned.1.call-start = ((), (), s32[]{:S(2)}) async-start(), calls=%async_computation.13 | async-start | bytes 2359296 | tf_op jit(solution)/shard_map/all_gather | solution.py:40
  11.2 116.4 %all-gather.17.cloned.1.call-start = ((), (), s32[]{:S(2)}) async-start(), calls=%async_computation.14 | async-start | bytes 2359296 | tf_op jit(solution)/shard_map/all_gather | solution.py:40
  13.2 152.3 %all-gather.21.cloned.1.call-start = ((), (), s32[]{:S(2)}) async-start(), calls=%async_computation.16 | async-start | bytes 2359296 | tf_op jit(solution)/shard_map/all_gather | solution.py:40
  13.8 189.5 %all-gather.23.cloned.1.call-start = ((), (), s32[]{:S(2)}) async-start(), calls=%async_computation.17 | async-start | bytes 2359296 | tf_op jit(solution)/shard_map/all_gather | solution.py:40
  14.5 226.7 %all-gather.19.cloned.1.call-start = ((), (), s32[]{:S(2)}) async-start(), calls=%async_computation.15 | async-start | bytes 2359296 | tf_op jit(solution)/shard_map/all_gather | solution.py:40
  15.1 353.3 %reduce-scatter.15.cloned.1.call-start = ((), (), s32[]{:S(2)}) async-start(), calls=%async_computation.10 | async-start | bytes 2359296 | tf_op jit(solution)/shard_map/reduce_scatter | solution.py:53
  18.1 109.5 %copy-start = (bf16[1,2048,512]{1,2,0:T(8,128)(2,1)}, bf16[1,2048,512]{1,2,0:T(8,128)(2,1)S(1)}, u32[]{:S(2)}) copy-start(bf16[1,2048,512]{1,2,0:T(8,128)(2,1)S(1)} %copy.20) | copy-start | bytes 6291460
  18.6 71.0 %copy-start.17 = (f32[2048]{0:T(1024)}, f32[2048]{0:T(1024)S(1)}, u32[]{:S(2)}) copy-start(f32[2048]{0:T(1024)S(1)} %add_rsqrt_fusion) | copy-start | bytes 24580
  137.8 65.5 %copy-start.7 = (bf16[2048,512]{0,1:T(8,128)(2,1)S(1)}, bf16[2048,512]{0,1:T(8,128)(2,1)}, u32[]{:S(2)}) copy-start(bf16[2048,512]{0,1:T(8,128)(2,1)} %get-tuple-element.27) | copy-start | bytes 6291460
  262.2 11.8 %copy-start.19 = (bf16[1,512,2048]{2,1,0:T(8,128)(2,1)S(1)}, bf16[1,512,2048]{2,1,0:T(8,128)(2,1)}, u32[]{:S(2)}) copy-start(bf16[1,512,2048]{2,1,0:T(8,128)(2,1)} %all-gather.19.cloned.1.call-done) | copy-start | bytes 6291460
  262.2 11.8 %copy-start.21 = (bf16[2048,2048]{1,0:T(8,128)(2,1)S(1)}, bf16[2048,2048]{1,0:T(8,128)(2,1)}, u32[]{:S(2)}) copy-start(bf16[2048,2048]{1,0:T(8,128)(2,1)} %get-tuple-element.28) | copy-start | bytes 25165828
  274.1 5.1 copy-start.2
  281.9 9.9 %copy-start.6 = (bf16[1,2048,512]{2,1,0:T(8,128)(2,1)S(1)}, bf16[1,2048,512]{2,1,0:T(8,128)(2,1)}, u32[]{:S(2)}) copy-start(bf16[1,2048,512]{2,1,0:T(8,128)(2,1)} %param.12) | copy-start | bytes 6291460
  291.7 78.0 %reduce-scatter.17.cloned.1.call-start = ((), (), s32[]{:S(2)}) async-start(), calls=%async_computation.11 | async-start | bytes 2359296 | tf_op jit(solution)/shard_map/reduce_scatter | solution.py:53
  306.4 10.3 %copy-start.1 = (bf16[1,2048,512]{1,2,0:T(8,128)(2,1)S(1)}, bf16[1,2048,512]{1,2,0:T(8,128)(2,1)}, u32[]{:S(2)}) copy-start(bf16[1,2048,512]{1,2,0:T(8,128)(2,1)} %copy-done) | copy-start | bytes 6291460
  306.4 10.3 %copy-start.18 = (f32[2048]{0:T(1024)S(1)}, f32[2048]{0:T(1024)}, u32[]{:S(2)}) copy-start(f32[2048]{0:T(1024)} %copy-done.17) | copy-start | bytes 24580
  306.4 103.5 %reduce-scatter.11.cloned.1.call-start = ((), (), s32[]{:S(2)}) async-start(), calls=%async_computation.8 | async-start | bytes 2359296 | tf_op jit(solution)/shard_map/reduce_scatter | solution.py:53
  327.3 122.4 %reduce-scatter.13.cloned.1.call-start = ((), (), s32[]{:S(2)}) async-start(), calls=%async_computation.9 | async-start | bytes 2359296 | tf_op jit(solution)/shard_map/reduce_scatter | solution.py:53
  340.5 149.6 %reduce-scatter.7.cloned.1.call-start = ((), (), s32[]{:S(2)}) async-start(), calls=%async_computation.6 | async-start | bytes 2359296 | tf_op jit(solution)/shard_map/reduce_scatter | solution.py:53
  358.3 192.7 %copy-start.3 = (bf16[2,256,512]{2,1,0:T(8,128)(2,1)S(1)}, bf16[2,256,512]{2,1,0:T(8,128)(2,1)}, u32[]{:S(2)}) copy-start(bf16[2,256,512]{2,1,0:T(8,128)(2,1)} %param.15) | copy-start | bytes 1572868
  358.3 172.0 %reduce-scatter.9.cloned.1.call-start = ((), (), s32[]{:S(2)}) async-start(), calls=%async_computation.7 | async-start | bytes 2359296 | tf_op jit(solution)/shard_map/reduce_scatter | solution.py:53
  368.4 186.3 %copy-start.4 = (bf16[2,64,2048]{2,1,0:T(8,128)(2,1)S(1)}, bf16[2,64,2048]{2,1,0:T(8,128)(2,1)}, u32[]{:S(2)}) copy-start(bf16[2,64,2048]{2,1,0:T(8,128)(2,1)} %param.13) | copy-start | bytes 1572868
  368.4 186.3 %copy-start.5 = (bf16[2,64,2048]{2,1,0:T(8,128)(2,1)S(1)}, bf16[2,64,2048]{2,1,0:T(8,128)(2,1)}, u32[]{:S(2)}) copy-start(bf16[2,64,2048]{2,1,0:T(8,128)(2,1)} %param.14) | copy-start | bytes 1572868
  368.4 186.3 %copy-start.9 = (f32[2,64,2048]{2,1,0:T(8,128)S(1)}, f32[2,64,2048]{2,1,0:T(8,128)}, u32[]{:S(2)}) copy-start(f32[2,64,2048]{2,1,0:T(8,128)} %param.19) | copy-start | bytes 3145732
  409.9 144.8 %copy-start.13 = (bf16[64,2048]{1,0:T(8,128)(2,1)S(1)}, bf16[64,2048]{1,0:T(8,128)(2,1)}, u32[]{:S(2)}) copy-start(bf16[64,2048]{1,0:T(8,128)(2,1)} %reduce-scatter.11.cloned.1.call-done) | copy-start | bytes 786436
  449.7 105.0 %copy-start.14 = (bf16[64,2048]{1,0:T(8,128)(2,1)S(1)}, bf16[64,2048]{1,0:T(8,128)(2,1)}, u32[]{:S(2)}) copy-start(bf16[64,2048]{1,0:T(8,128)(2,1)} %reduce-scatter.13.cloned.1.call-done) | copy-start | bytes 786436
  490.2 64.6 %copy-start.15 = (bf16[64,2048]{1,0:T(8,128)(2,1)S(1)}, bf16[64,2048]{1,0:T(8,128)(2,1)}, u32[]{:S(2)}) copy-start(bf16[64,2048]{1,0:T(8,128)(2,1)} %reduce-scatter.7.cloned.1.call-done) | copy-start | bytes 786436
  551.0 3.8 copy-start.10
  551.0 3.7 copy-start.11
  551.0 3.7 copy-start.12
  551.0 3.7 copy-start.16
  (2 other events, 4.6 us)
Sparse Core Ops, SparseCore 0:
  10.2 41.3 all-gather.12
  53.7 35.8 all-gather.14
  91.7 35.8 all-gather.16
  129.6 35.8 all-gather.20
  167.4 35.8 all-gather.22
  205.3 35.8 all-gather.18
  291.8 37.4 reduce-scatter.14
  331.7 37.9 reduce-scatter.16
  372.0 37.8 reduce-scatter.10
  412.1 37.6 reduce-scatter.12
  452.1 38.0 reduce-scatter.6
  492.4 37.8 reduce-scatter.8
where the time goes:
time: 572 us; the launch traced here: 565 us
  waiting for transfers between devices  323 us (56%)
  matrix products  176 us (31%)
  between operations  17.6 us (3%)
  local copies, waits for them, and re-layouts  17.4 us (3%)
  blocking collectives  16.1 us (3%)
  other arithmetic  14.3 us (2%)
    all_gather x6, waiting for transfers between devices, fetched(): lax.all_gather(w[number], 'dp', axis=0, tiled=True)  162 us
    reduce_scatter x6, waiting for transfers between devices, step(): lax.psum_scatter(by_w[name], 'dp', scatter_dimension=0, tiled=True)  158 us
    dot_general x5, matrix products, layer(): gate = jnp.dot(a, w['w_gate'], preferred_element_type=jnp.float32)  63.4 us
    dot_general x5, matrix products, layer(): up = jnp.dot(a, w['w_up'], preferred_element_type=jnp.float32)  61.3 us
    dot_general x5, matrix products, matmul(): jnp.dot(a, w, preferred_element_type=jnp.float32).astype(jnp.bfloat16)  51.5 us
    psum x1, blocking collectives, step(): squares = lax.psum(sum((jnp.sum(g * g) for g in gradients)), 'dp')  16.1 us
    unnamed x46, local copies, waits for them, and re-layouts  11.9 us
  transfers between devices with their start and end apart: 12, of which 11 were waited for; matrix products, arithmetic and copies ran while one was open for 25% of the time, Pallas kernels for 0%

commit v1 on v0

v1 whole, which is shorter than its diff:
```python
import functools
import math

import jax
import jax.numpy as jnp
from jax import lax
from jax.experimental import pallas as pl
from jax.experimental.pallas import tpu as pltpu
from jax.sharding import PartitionSpec as P

MESH = pl.DeviceIdType.MESH
F32, BF16 = jnp.float32, jnp.bfloat16
CHUNKS = 4
SPACING = 4
PHASE = 8


def dot(a, b):
    return jnp.dot(a, b, preferred_element_type=F32)


def dot_t(a, b):
    return lax.dot_general(a, b, (((1,), (1,)), ((), ())), preferred_element_type=F32)


def sigmoid(x):
    return 0.5 * jnp.tanh(0.5 * x) + 0.5


def scale_of(wide):
    return lax.rsqrt(jnp.mean(wide * wide, -1, keepdims=True) + 1e-6)


def span(start, size):
    return pl.ds(pl.multiple_of(start, size), size)


def kernel(
    n,
    across,
    x_in,
    dy_in,
    wg_in,
    wu_in,
    wd_in,
    gu_out,
    gd_out,
    factor_out,
    wgu,
    wd,
    gu,
    gd,
    land_gu,
    land_gd,
    xs,
    do,
    h1,
    a,
    at,
    dot_do,
    big,
    acc,
    squares_gu,
    squares_gd,
    all_squares,
    load_sem,
    out_sem,
    ag_send,
    ag_z,
    ag_pair,
    ag_core,
    rs_send,
    rs_recv,
    sq_send,
    sq_recv,
):
    tokens, d = xs.shape
    ff = wgu.shape[3]
    own_d, own_f = d // n, ff // n
    fc = ff // CHUNKS
    me, rep = lax.axis_index("dp"), lax.axis_index("rep")
    core, y_bit, x_bit = rep % 2, (rep // 2) % 2, (rep // (2 * across)) % 2
    parity = (x_bit + y_bit) % 2

    def around(k):
        return lax.rem(me + (k + n), n)

    right, left = {"dp": around(1)}, {"dp": around(-1)}
    other_core = {"rep": rep + 1 - 2 * core}
    other_y = {"rep": rep + 2 - 4 * y_bit}
    other_x = {"rep": rep + 2 * across * (1 - 2 * x_bit)}

    barrier = pltpu.get_barrier_semaphore()
    partners = [{"dp": around(k)} for k in range(1, n)] + [other_core, other_y, other_x]
    for partner in partners:
        pl.semaphore_signal(barrier, inc=1, device_id=partner, device_id_type=MESH)

    loads = []
    for number in range(2):
        loads.append(pltpu.make_async_copy(wg_in.at[number], wgu.at[number, 0, span(me * own_d, own_d), :], load_sem.at[number, 0]))
        loads.append(pltpu.make_async_copy(wu_in.at[number], wgu.at[number, 1, span(me * own_d, own_d), :], load_sem.at[number, 1]))
        loads.append(pltpu.make_async_copy(wd_in.at[number], wd.at[number, span(me * own_f, own_f), :], load_sem.at[number, 2]))
    load_x = pltpu.make_async_copy(x_in.at[0], xs, load_sem.at[0, 3])
    load_dy = pltpu.make_async_copy(dy_in.at[0], do, load_sem.at[1, 3])
    for load in loads[:3] + [load_x] + loads[3:] + [load_dy]:
        load.start()
    pl.semaphore_wait(barrier, len(partners))

    eighth_f, eighth_r = ff // 8, own_f // 8
    mine = 4 * core + 2 * parity
    theirs = 4 * core + 2 * (1 - parity)

    def part(kind, number, shard, eighth, count):
        if kind == 0:
            return wgu.at[number, :, span(shard * own_d, own_d), pl.ds(pl.multiple_of(eighth * eighth_f, eighth_f), count * eighth_f)]
        return wd.at[number, pl.ds(pl.multiple_of(shard * own_f + eighth * eighth_r, eighth_r), count * eighth_r), :]

    def bytes_of(kind, number, eighths):
        if kind == 0:
            return wgu.at[number, :, pl.ds(0, eighths * own_d // 8), :]
        return wd.at[number, pl.ds(0, eighths * eighth_r), :]

    def await_eighths(kind, number, eighths, sem):
        ref = bytes_of(kind, number, eighths)
        pltpu.make_async_copy(ref, ref, sem).wait()

    def push(kind, number, shard, eighth, count, recv_sem, device):
        ref = part(kind, number, shard, eighth, count)
        pltpu.make_async_remote_copy(
            src_ref=ref, dst_ref=ref, send_sem=ag_send.at[kind, number], recv_sem=recv_sem, device_id=device, device_id_type=MESH
        ).start()

    def gather_round(kind, number, r):
        core_sem = ag_core.at[kind, number]
        if r >= 1 and r <= 4:
            await_eighths(kind, number, 4 if r <= 3 else 2, ag_z.at[kind, number, r - 1])
        if r <= 2:
            push(kind, number, around(-r), mine, 2, ag_z.at[kind, number, r], right)
            push(kind, number, around(r), mine, 2, ag_z.at[kind, number, r], left)
        elif r == 3:
            push(kind, number, around(-r), mine, 1, ag_z.at[kind, number, r], right)
            push(kind, number, around(r), mine + 1, 1, ag_z.at[kind, number, r], left)
        if r >= 1 and r <= 4:
            for shard in (around(-r), around(r)) if r <= 3 else (around(r),):
                push(kind, number, shard, mine, 1, ag_pair.at[kind, number, r - 1], other_y)
                push(kind, number, shard, mine + 1, 1, ag_pair.at[kind, number, r - 1], other_x)
                push(kind, number, shard, mine, 2, core_sem, other_core)
        if r >= 2:
            s = r - 1
            await_eighths(kind, number, 4 if s <= 3 else 2, ag_pair.at[kind, number, s - 1])
            for shard in (around(-s), around(s)) if s <= 3 else (around(s),):
                push(kind, number, shard, theirs, 2, core_sem, other_core)

    def gathered(kind, number):
        await_eighths(kind, number, 28, ag_core.at[kind, number])

    half_d = own_d // 2
    rows_d = d // 2
    half_r = rows_d // 2
    sides = ((right, 1), (left, -1))

    def wait_for(ref, sem):
        pltpu.make_async_copy(ref, ref, sem).wait()

    def hop(lam, q, s, group, block_of, half_of, slot_of, slot_half_of, final):
        for side, (device, sign) in enumerate(sides):
            send, recv = rs_send.at[group, side], rs_recv.at[group, side]
            block = lax.rem(me + sign * (4 - s) + n, n)

            def go(src, dst, step, send=send, recv=recv, device=device):
                pltpu.make_async_remote_copy(
                    src_ref=src, dst_ref=dst, send_sem=send, recv_sem=recv.at[step], device_id=device, device_id_type=MESH
                ).start()

            @pl.when(s == 0)
            def _(side=side, block=block, go=go):
                go(half_of(block, side), slot_half_of(side, 0, side), 0)

            @pl.when(s == 1)
            def _(side=side, block=block, go=go, send=send, recv=recv):
                wait_for(slot_half_of(side, 0, side), send)
                wait_for(slot_half_of(side, 0, side), recv.at[0])
                total, arrived = half_of(block, side), slot_half_of(side, 0, side)
                total[...] = (total[...].astype(F32) + arrived[...].astype(F32)).astype(BF16)
                go(block_of(block), slot_of(side, 1), 1)

            @pl.when((s == 2) | (s == 3))
            def _(side=side, block=block, go=go, send=send, recv=recv):
                wait_for(slot_of(side, s - 1), send)
                wait_for(slot_of(side, s - 1), recv.at[s - 1])
                total, arrived = block_of(block), slot_of(side, s - 1)
                total[...] = (total[...].astype(F32) + arrived[...].astype(F32)).astype(BF16)
                go(block_of(block), slot_of(side, s), s)

        @pl.when(s == 4)
        def _():
            for side in range(2):
                wait_for(slot_of(side, 3), rs_send.at[group, side])
                wait_for(slot_of(side, 3), rs_recv.at[group, side, 3])
            total, first, second = block_of(me), slot_of(0, 3), slot_of(1, 3)
            whole = (total[...].astype(F32) + first[...].astype(F32) + second[...].astype(F32)).astype(BF16)
            total[...] = whole
            final(whole.astype(F32))

    def hop_gu(lam, q, s):
        cols = span(q * fc, fc)

        def add_squares(g):
            squares_gu[...] += jnp.sum((g * g).reshape(-1, 8, fc), axis=0)

        hop(
            lam,
            q,
            s,
            q,
            lambda b: gu.at[lam, :, span(b * own_d, own_d), cols],
            lambda b, half: gu.at[lam, :, span(b * own_d + half * half_d, half_d), cols],
            lambda side, step: land_gu.at[q, side, step],
            lambda side, step, half: land_gu.at[q, side, step, :, pl.ds(half * half_d, half_d), :],
            add_squares,
        )

    def hop_gd(lam, h, s):
        def add_squares(g):
            squares_gd[...] += jnp.sum((g * g).reshape(-1, 8, own_f), axis=0)

        hop(
            lam,
            h,
            s,
            CHUNKS + h,
            lambda b: gd.at[lam, span(h * rows_d, rows_d), span(b * own_f, own_f)],
            lambda b, half: gd.at[lam, span(h * rows_d + half * half_r, half_r), span(b * own_f, own_f)],
            lambda side, step: land_gd.at[h, side, step],
            lambda side, step, half: land_gd.at[h, side, step, pl.ds(half * half_r, half_r), :],
            add_squares,
        )

    def tick(t):
        period = CHUNKS * PHASE

        def one(q, start, run):
            u = t - start
            s = lax.rem(jnp.maximum(u, 0), period)

            @pl.when((u >= 0) & (u < 2 * period) & (lax.rem(s, SPACING) == 0) & (s < 5 * SPACING))
            def _():
                run(lax.div(jnp.maximum(u, 0), period), q, lax.div(s, SPACING))

        def quarter(q, _):
            one(q, PHASE * (q + 1), hop_gu)
            return 0

        lax.fori_loop(0, CHUNKS, quarter, 0)

        def half(h, _):
            one(h, period + 1 + h, hop_gd)
            return 0

        lax.fori_loop(0, 2, half, 0)

    squares_gu[...] = jnp.zeros_like(squares_gu)
    squares_gd[...] = jnp.zeros_like(squares_gd)
    tm = tokens // 8
    tb = tokens // 4

    def norm_rows(i, src):
        rows = span(i * tm, tm)
        wide = src[rows, :].astype(F32)
        a[rows, :] = (wide * scale_of(wide)).astype(BF16)

    def transpose_rows(i, src, dst):
        rows = span(i * tm, tm)
        dst[:, rows] = src[rows, :].astype(F32).T.astype(BF16)

    for load in loads[:3]:
        load.wait()
    gather_round(0, 0, 0)
    gather_round(1, 0, 0)
    load_x.wait()
    lax.fori_loop(0, 8, lambda i, _: (norm_rows(i, xs), 0)[1], 0)
    gather_round(0, 0, 1)
    gather_round(1, 0, 1)
    load_dy.wait()
    lax.fori_loop(0, 8, lambda i, _: (transpose_rows(i, do, dot_do), 0)[1], 0)
    for r in (2, 3, 4):
        gather_round(0, 0, r)
        gather_round(1, 0, r)
    for load in loads[3:]:
        load.wait()
    gather_round(0, 1, 0)
    gather_round(1, 1, 0)
    gather_round(0, 0, 5)
    gathered(0, 0)
    gather_round(1, 0, 5)

    def hidden(i, _):
        rows = span(i * tm, tm)
        here = a[rows, :]
        for c in range(CHUNKS):
            cols = slice(c * fc, (c + 1) * fc)
            gate, up = dot(here, wgu[0, 0, :, cols]), dot(here, wgu[0, 1, :, cols])
            big[rows, cols] = (gate * sigmoid(gate) * up).astype(BF16)
        return 0

    lax.fori_loop(0, 2, hidden, 0)
    gather_round(0, 1, 1)
    gather_round(1, 1, 1)
    lax.fori_loop(2, 4, hidden, 0)
    gather_round(0, 1, 2)
    gather_round(1, 1, 2)
    lax.fori_loop(4, 6, hidden, 0)
    gather_round(0, 1, 3)
    gather_round(1, 1, 3)
    lax.fori_loop(6, 8, hidden, 0)
    gathered(1, 0)

    def down(i, _):
        rows = span(i * tm, tm)
        h = (xs[rows, :].astype(F32) + dot(big[rows, :], wd[0]).astype(BF16).astype(F32)).astype(BF16)
        h1[rows, :] = h
        wide = h.astype(F32)
        normed = wide * scale_of(wide)
        a[rows, :] = normed.astype(BF16)
        at[:, rows] = normed.astype(BF16).astype(F32).T.astype(BF16)
        return 0

    lax.fori_loop(0, 3, down, 0)
    gather_round(0, 1, 4)
    gather_round(1, 1, 4)
    lax.fori_loop(3, 8, down, 0)
    gather_round(0, 1, 5)
    gather_round(1, 1, 5)
    gathered(0, 1)
    gathered(1, 1)

    act_cols, gate_cols, up_cols = (slice(k * fc, (k + 1) * fc) for k in range(3))

    for lam in range(2):
        number = 1 - lam

        def quarter(c, _, lam=lam, number=number):
            cols = span(c * fc, fc)
            t0 = (lam * CHUNKS + c) * PHASE

            def rows_of(i, _):
                rows = span(i * tb, tb)
                here = a[rows, :]
                gate, up = dot(here, wgu[number, 0, :, cols]), dot(here, wgu[number, 1, :, cols])
                by_act = dot_t(do[rows, :], wd[number, cols, :]).astype(BF16).astype(F32)
                sig = sigmoid(gate)
                silu = gate * sig
                big[rows, act_cols] = (silu * up).astype(BF16)
                big[rows, up_cols] = (by_act * silu).astype(BF16)
                big[rows, gate_cols] = (by_act * up * (sig + silu * (1.0 - sig))).astype(BF16)
                tick(t0 + i)
                return 0

            lax.fori_loop(0, 4, rows_of, 0)
            gu[lam, 0, :, cols] = dot(at[...], big[:, gate_cols]).astype(BF16)
            tick(t0 + 4)
            gu[lam, 1, :, cols] = dot(at[...], big[:, up_cols]).astype(BF16)
            tick(t0 + 5)
            gd[lam, :, cols] = dot(dot_do[...], big[:, act_cols]).astype(BF16)
            tick(t0 + 6)
            if lam == 0:

                def by_input(i, _):
                    rows = span(i * tb, tb)
                    by_a = dot_t(big[rows, gate_cols], wgu[number, 0, :, cols]) + dot_t(big[rows, up_cols], wgu[number, 1, :, cols])

                    @pl.when(c == 0)
                    def _():
                        acc[rows, :] = by_a

                    @pl.when(c > 0)
                    def _():
                        acc[rows, :] += by_a

                    return 0

                lax.fori_loop(0, 4, by_input, 0)
            tick(t0 + 7)
            return 0

        lax.fori_loop(0, CHUNKS, quarter, 0)

        if lam == 0:

            def through_norm(i, _):
                rows = span(i * tm, tm)
                by_a = acc[rows, :].astype(BF16).astype(F32)
                wide = h1[rows, :].astype(F32)
                scale = scale_of(wide)
                inner = jnp.mean(by_a * wide, -1, keepdims=True)
                by_h = (by_a * scale - wide * (scale * scale * scale * inner)).astype(BF16).astype(F32)
                by_h = (do[rows, :].astype(F32) + by_h).astype(BF16)
                do[rows, :] = by_h
                dot_do[:, rows] = by_h.astype(F32).T.astype(BF16)
                wide = xs[rows, :].astype(F32)
                normed = (wide * scale_of(wide)).astype(BF16)
                a[rows, :] = normed
                at[:, rows] = normed.astype(F32).T.astype(BF16)
                return 0

            lax.fori_loop(0, 8, through_norm, 0)

    last = 2 * CHUNKS * PHASE + 4 * SPACING + 3
    lax.fori_loop(2 * CHUNKS * PHASE, last, lambda t, _: (tick(t), 0)[1], 0)

    outs = []
    for lam in range(2):
        outs.append(pltpu.make_async_copy(gu.at[lam, :, span(me * own_d, own_d), :], gu_out.at[1 - lam], out_sem.at[lam, 0]))
        outs.append(pltpu.make_async_copy(gd.at[lam, :, span(me * own_f, own_f)], gd_out.at[1 - lam], out_sem.at[lam, 1]))
    for out in outs:
        out.start()
    lanes = all_squares.shape[2]
    tile = sum(squares_gu[:, i * lanes : (i + 1) * lanes] for i in range(fc // lanes))
    tile = tile + sum(squares_gd[:, i * lanes : (i + 1) * lanes] for i in range(own_f // lanes))
    all_squares[me] = tile
    copies = [
        pltpu.make_async_remote_copy(
            src_ref=all_squares.at[me],
            dst_ref=all_squares.at[me],
            send_sem=sq_send.at[k - 1],
            recv_sem=sq_recv.at[k - 1],
            device_id={"dp": around(k)},
            device_id_type=MESH,
        )
        for k in range(1, n)
    ]
    for copy in copies:
        copy.start()
    for copy in copies:
        copy.wait()
    total = jnp.sum(all_squares[...])
    count = n * (gu_out.size + gd_out.size)
    factor_out[...] = jnp.minimum(1.0, 0.5 * lax.rsqrt(jnp.full(factor_out.shape, total, F32) / count + 1e-30))
    for kind in range(2):
        for number in range(2):
            await_eighths(kind, number, 56, ag_send.at[kind, number])
    for out in outs:
        out.wait()


def adamw(w, m, v, g):
    m = 0.9 * m + 0.1 * g
    v = 0.95 * v + 0.05 * g * g
    step = m * lax.rsqrt(v + 1e-8) + 0.1 * w
    return (w - 0.02 * step).astype(jnp.bfloat16), m, v


def solution(mesh):
    n, groups = mesh.shape["dp"], mesh.shape["rep"]
    across = math.isqrt(groups // 2)

    def step(x, dy, *arrays):
        weights, m, v = (arrays[i : i + 3] for i in (0, 3, 6))
        layers, own_d, ff = weights[0].shape
        own_f, d = weights[2].shape[1:]
        tokens = x.shape[1]
        fc = ff // CHUNKS
        lanes = min(128, own_f)
        anywhere = pl.BlockSpec(memory_space=pl.ANY)
        grads_gu, grads_gd, factor = pl.pallas_call(
            functools.partial(kernel, n, across),
            out_shape=(
                jax.ShapeDtypeStruct((layers, 2, own_d, ff), BF16),
                jax.ShapeDtypeStruct((layers, d, own_f), BF16),
                jax.ShapeDtypeStruct((8, lanes), F32),
            ),
            in_specs=[anywhere] * 5,
            out_specs=(anywhere, anywhere, pl.BlockSpec(memory_space=pltpu.VMEM)),
            scratch_shapes=[
                pltpu.VMEM((layers, 2, d, ff), BF16),
                pltpu.VMEM((layers, ff, d), BF16),
                pltpu.VMEM((layers, 2, d, ff), BF16),
                pltpu.VMEM((layers, d, ff), BF16),
                pltpu.VMEM((CHUNKS, 2, 4, 2, own_d, fc), BF16),
                pltpu.VMEM((2, 2, 4, d // 2, own_f), BF16),
                pltpu.VMEM((tokens, d), BF16),
                pltpu.VMEM((tokens, d), BF16),
                pltpu.VMEM((tokens, d), BF16),
                pltpu.VMEM((tokens, d), BF16),
                pltpu.VMEM((d, tokens), BF16),
                pltpu.VMEM((d, tokens), BF16),
                pltpu.VMEM((tokens, ff), BF16),
                pltpu.VMEM((tokens, d), F32),
                pltpu.VMEM((8, fc), F32),
                pltpu.VMEM((8, own_f), F32),
                pltpu.VMEM((n, 8, lanes), F32),
                pltpu.SemaphoreType.DMA((2, 4)),
                pltpu.SemaphoreType.DMA((2, 2)),
                pltpu.SemaphoreType.DMA((2, 2)),
                pltpu.SemaphoreType.DMA((2, 2, 4)),
                pltpu.SemaphoreType.DMA((2, 2, 4)),
                pltpu.SemaphoreType.DMA((2, 2)),
                pltpu.SemaphoreType.DMA((CHUNKS + 2, 2)),
                pltpu.SemaphoreType.DMA((CHUNKS + 2, 2, 4)),
                pltpu.SemaphoreType.DMA((n - 1,)),
                pltpu.SemaphoreType.DMA((n - 1,)),
            ],
            compiler_params=pltpu.CompilerParams(collective_id=0, has_side_effects=True, vmem_limit_bytes=67043328),
            name="train_step",
        )(x, dy, *weights)
        factor = factor[0, 0]
        gradients = [grads_gu[:, 0], grads_gu[:, 1], jnp.swapaxes(grads_gd, 1, 2)]
        new = [adamw(w.astype(F32), m, v, g.astype(F32) * factor) for w, m, v, g in zip(weights, m, v, gradients, strict=True)]
        return tuple(one[which] for which in range(3) for one in new)

    states, cut = P(("rep", "dp"), None, None), P(None, "dp", None)
    return jax.shard_map(
        step,
        mesh=mesh,
        in_specs=(states, states) + (cut,) * 9,
        out_specs=(P("rep", "dp", None),) * 9,
        check_vma=False,
    )
```

time: 572 us -> 243 us (0.42); the launches traced: 565 us -> 243 us
  waiting for transfers between devices: 323 us -> 0 us
  Pallas kernels: 0 us -> 224 us
  matrix products: 176 us -> 0 us
  between operations: 17.6 us -> 0.67 us
  blocking collectives: 16.1 us -> 0 us
  local copies, waits for them, and re-layouts: 17.4 us -> 8.68 us
    pallas_call x0 -> x1, Pallas kernels: none -> 224 us  [step(): pl.pallas_call(functools.partial(kernel, n, across), out_shape=(jax.Shape...]
    dot_general x15 -> x0, matrix products: 176 us -> none  [the longest x5 63.4 us: layer(): gate = jnp.dot(a, w['w_gate'], preferred_element_type=jnp.float32)]
    all_gather x6 -> x0, waiting for transfers between devices: 162 us -> none  [fetched(): lax.all_gather(w[number], 'dp', axis=0, tiled=True)]
    reduce_scatter x6 -> x0, waiting for transfers between devices: 158 us -> none  [step(): lax.psum_scatter(by_w[name], 'dp', scatter_dimension=0, tiled=True)]
    psum x1 -> x0, blocking collectives: 16.1 us -> none  [step(): squares = lax.psum(sum((jnp.sum(g * g) for g in gradients)), 'dp')]
    reduce_sum x4 -> x0, other arithmetic: 6.2 us -> none  [the longest x3 5.75 us: step(): squares = lax.psum(sum((jnp.sum(g * g) for g in gradients)), 'dp')]
    unnamed x46 -> x12, local copies, waits for them, and re-layouts: 11.9 us -> 7.49 us
  transfers between devices with their start and end apart: 12 -> 0, of which waited for: 11 -> 0; matrix products, arithmetic and copies ran while one was open for 25% -> 0% of each run, Pallas kernels for 0% -> 0%
where the time goes in v1:
time: 243 us
  Pallas kernels  224 us (92%)
  other arithmetic  10.1 us (4%)
  local copies, waits for them, and re-layouts  8.68 us (4%)
    pallas_call x1, Pallas kernels, step(): pl.pallas_call(functools.partial(kernel, n, across), out_shape=(jax.Shape...  224 us
    convert_element_type x2, other arithmetic, adamw(): return ((w - 0.02 * step).astype(jnp.bfloat16), m, v)  10.1 us
    unnamed x12, local copies, waits for them, and re-layouts  7.49 us

profile of v1, /device:TPU:22, one launch (start us, length us, event | category | flops | bytes accessed | tf_op | source)
XLA Modules:
  0.0 243.0 jit_solution(15369660887701298944)
XLA Ops:
  0.6 223.6 %train_step.1 = (bf16[2,2,64,2048]{3,2,1,0:T(8,128)(2,1)}, bf16[2,512,256]{2,1,0:T(8,128)(2,1)}, f32[8,128]{1,0:T(8,128)}) custom-call(bf16[1,2048,512]{2,1,0:T(8,128)(2,1)} %x_in.1, bf16[1,2048,512]{2,1,0:T(8,128)(2,1)} %dy_in.1, bf16[2,64,2048]{2,1,0:T(8,128)(2,1)} %wg_in.1, bf16[2,64,2048]{2,1,0:T(8,128)(2,1)} %wu_in.1, bf16[2,256,512]{2,1,0:T(8,128)(2,1)} %wd_in.1), custom_call_target="tpu_custom_call" | custom-call | tf_op jit(solution)/shard_map/train_step/pallas_call | solution.py:465
  224.2 1.2 slice.10
  225.4 0.0 copy-start.2
  225.4 6.5 %fusion.2 = (bf16[2,64,2048]{2,1,0:T(8,128)(2,1)}, f32[2,64,2048]{2,1,0:T(8,128)}, f32[2,64,2048]{2,1,0:T(8,128)}, bf16[2,64,2048]{2,1,0:T(8,128)(2,1)}, f32[2,64,2048]{2,1,0:T(8,128)}, /*index=5*/f32[2,64,2048]{2,1,0:T(8,128)}) fusion(bf16[2,64,2048]{2,1,0:T(8,128)(2,1)} %wg_in.1, f32[]{:T(128)} %bitcast, f32[2,64,2048]{2,1,0:T(8,128)} %param.19, ...), kind=kLoop, calls=%fused_computation.11 | loop fusion | flops 8912896 | bytes 11534340 | tf_op jit(solution)/shard_map/convert_element_type | solution.py:450
  231.9 0.0 copy-done.2
  231.9 0.0 copy-start.1
  231.9 0.3 copy.23
  232.2 2.5 %copy.24 = f32[2,256,512]{1,2,0:T(8,128)} copy(f32[2,256,512]{2,1,0:T(8,128)} %param.21) | data formatting | bytes 2097152 | tf_op args[10]
  234.8 0.0 copy-done.1
  234.8 1.0 copy.22
  235.8 3.6 %fusion.8 = (bf16[2,256,512]{1,2,0:T(8,128)(2,1)}, f32[2,256,512]{1,2,0:T(8,128)S(1)}, f32[2,256,512]{1,2,0:T(8,128)S(1)}) fusion(bf16[2,256,512]{1,2,0:T(8,128)(2,1)} %copy.22, f32[]{:T(128)} %bitcast, bf16[2,512,256]{2,1,0:T(8,128)(2,1)} %get-tuple-element.14, f32[2,256,512]{1,2,0:T(8,128)} %copy.24, f32[2,256,512]{1,2,0:T(8,128)S(1)} %copy.23), kind=kLoop, calls=%fused_computation.17 | loop fusion | flops 4456448 | bytes 5767172 | tf_op jit(solution)/shard_map/convert_element_type | solution.py:450
  239.4 0.0 copy-start
  239.4 1.3 copy.26
  240.7 1.3 copy.27
  242.0 0.0 copy-done
  242.0 1.0 copy.25
Async XLA Ops:
  225.4 6.5 %copy-start.2 = (f32[2,256,512]{2,1,0:T(8,128)S(1)}, f32[2,256,512]{2,1,0:T(8,128)}, u32[]{:S(2)}) copy-start(f32[2,256,512]{2,1,0:T(8,128)} %param.18) | copy-start | bytes 3145732
  231.9 2.9 %copy-start.1 = (bf16[2,256,512]{2,1,0:T(8,128)(2,1)S(1)}, bf16[2,256,512]{2,1,0:T(8,128)(2,1)}, u32[]{:S(2)}) copy-start(bf16[2,256,512]{2,1,0:T(8,128)(2,1)} %wd_in.1) | copy-start | bytes 1572868
  239.4 2.6 %copy-start = (bf16[2,256,512]{1,2,0:T(8,128)(2,1)S(1)}, bf16[2,256,512]{1,2,0:T(8,128)(2,1)}, u32[]{:S(2)}) copy-start(bf16[2,256,512]{1,2,0:T(8,128)(2,1)} %get-tuple-element.24) | copy-start | bytes 1572868

commit v2 on v1

--- a/solution.py
+++ b/solution.py
@@ -11,8 +11,10 @@
 MESH = pl.DeviceIdType.MESH
 F32, BF16 = jnp.float32, jnp.bfloat16
 CHUNKS = 4
-SPACING = 4
+SPACING = 5
 PHASE = 8
+START = 5
+PERIOD = (CHUNKS + 1) * PHASE
 
 
 def dot(a, b):
@@ -43,8 +45,9 @@
     wg_in,
     wu_in,
     wd_in,
-    gu_out,
-    gd_out,
+    g_out,
+    u_out,
+    d_out,
     factor_out,
     wgu,
     wd,
@@ -58,8 +61,9 @@
     a,
     at,
     dot_do,
-    big,
-    acc,
+    act,
+    by_gu,
+    d_own,
     squares_gu,
     squares_gd,
     all_squares,
@@ -111,13 +115,13 @@
     theirs = 4 * core + 2 * (1 - parity)
 
     def part(kind, number, shard, eighth, count):
-        if kind == 0:
-            return wgu.at[number, :, span(shard * own_d, own_d), pl.ds(pl.multiple_of(eighth * eighth_f, eighth_f), count * eighth_f)]
+        if kind < 2:
+            return wgu.at[number, kind, span(shard * own_d, own_d), pl.ds(pl.multiple_of(eighth * eighth_f, eighth_f), count * eighth_f)]
         return wd.at[number, pl.ds(pl.multiple_of(shard * own_f + eighth * eighth_r, eighth_r), count * eighth_r), :]
 
     def bytes_of(kind, number, eighths):
-        if kind == 0:
-            return wgu.at[number, :, pl.ds(0, eighths * own_d // 8), :]
+        if kind < 2:
+            return wgu.at[number, kind, pl.ds(0, eighths * own_d // 8), :]
         return wd.at[number, pl.ds(0, eighths * eighth_r), :]
 
     def await_eighths(kind, number, eighths, sem):
@@ -174,13 +178,13 @@
 
             @pl.when(s == 0)
             def _(side=side, block=block, go=go):
-                go(half_of(block, side), slot_half_of(side, 0, side), 0)
+                go(half_of(block, side), slot_half_of(side), 0)
 
             @pl.when(s == 1)
             def _(side=side, block=block, go=go, send=send, recv=recv):
-                wait_for(slot_half_of(side, 0, side), send)
-                wait_for(slot_half_of(side, 0, side), recv.at[0])
-                total, arrived = half_of(block, side), slot_half_of(side, 0, side)
+                wait_for(slot_half_of(side), send)
+                wait_for(slot_half_of(side), recv.at[0])
+                total, arrived = half_of(block, side), slot_half_of(side)
                 total[...] = (total[...].astype(F32) + arrived[...].astype(F32)).astype(BF16)
                 go(block_of(block), slot_of(side, 1), 1)
 
@@ -199,13 +203,14 @@
                 wait_for(slot_of(side, 3), rs_recv.at[group, side, 3])
             total, first, second = block_of(me), slot_of(0, 3), slot_of(1, 3)
             whole = (total[...].astype(F32) + first[...].astype(F32) + second[...].astype(F32)).astype(BF16)
-            total[...] = whole
-            final(whole.astype(F32))
+            final(total, whole)
 
     def hop_gu(lam, q, s):
         cols = span(q * fc, fc)
 
-        def add_squares(g):
+        def finish(total, whole):
+            total[...] = whole
+            g = whole.astype(F32)
             squares_gu[...] += jnp.sum((g * g).reshape(-1, 8, fc), axis=0)
 
         hop(
@@ -215,13 +220,15 @@
             q,
             lambda b: gu.at[lam, :, span(b * own_d, own_d), cols],
             lambda b, half: gu.at[lam, :, span(b * own_d + half * half_d, half_d), cols],
-            lambda side, step: land_gu.at[q, side, step],
-            lambda side, step, half: land_gu.at[q, side, step, :, pl.ds(half * half_d, half_d), :],
-            add_squares,
+            lambda side, step: land_gu.at[q, side, :, pl.ds(pl.multiple_of((2 * step - 1) * half_d, half_d), own_d), :],
+            lambda side: land_gu.at[q, side, :, pl.ds(0, half_d), :],
+            finish,
         )
 
     def hop_gd(lam, h, s):
-        def add_squares(g):
+        def finish(total, whole):
+            g = whole.astype(F32)
+            d_own[lam, :, span(h * rows_d, rows_d)] = g.T.astype(BF16)
             squares_gd[...] += jnp.sum((g * g).reshape(-1, 8, own_f), axis=0)
 
         hop(
@@ -231,30 +238,28 @@
             CHUNKS + h,
             lambda b: gd.at[lam, span(h * rows_d, rows_d), span(b * own_f, own_f)],
             lambda b, half: gd.at[lam, span(h * rows_d + half * half_r, half_r), span(b * own_f, own_f)],
-            lambda side, step: land_gd.at[h, side, step],
-            lambda side, step, half: land_gd.at[h, side, step, pl.ds(half * half_r, half_r), :],
-            add_squares,
+            lambda side, step: land_gd.at[h, side, pl.ds(pl.multiple_of((2 * step - 1) * half_r, half_r), rows_d), :],
+            lambda side: land_gd.at[h, side, pl.ds(0, half_r), :],
+            finish,
         )
 
     def tick(t):
-        period = CHUNKS * PHASE
-
         def one(q, start, run):
             u = t - start
-            s = lax.rem(jnp.maximum(u, 0), period)
-
-            @pl.when((u >= 0) & (u < 2 * period) & (lax.rem(s, SPACING) == 0) & (s < 5 * SPACING))
+            s = lax.rem(jnp.maximum(u, 0), PERIOD)
+
+            @pl.when((u >= 0) & (u < 2 * PERIOD) & (lax.rem(s, SPACING) == 0) & (s < 5 * SPACING))
             def _():
-                run(lax.div(jnp.maximum(u, 0), period), q, lax.div(s, SPACING))
+                run(lax.div(jnp.maximum(u, 0), PERIOD), q, lax.div(s, SPACING))
 
         def quarter(q, _):
-            one(q, PHASE * (q + 1), hop_gu)
+            one(q, PHASE * q + START, hop_gu)
             return 0
 
         lax.fori_loop(0, CHUNKS, quarter, 0)
 
         def half(h, _):
-            one(h, period + 1 + h, hop_gd)
+            one(h, PHASE * CHUNKS + h, hop_gd)
             return 0
 
         lax.fori_loop(0, 2, half, 0)
@@ -273,123 +278,111 @@
         rows = span(i * tm, tm)
         dst[:, rows] = src[rows, :].astype(F32).T.astype(BF16)
 
+    def rounds(number, r, kinds=(0, 1, 2)):
+        for kind in kinds:
+            gather_round(kind, number, r)
+
+    def loop(first, end, body):
+        lax.fori_loop(first, end, lambda i, _: (body(i), 0)[1], 0)
+
     for load in loads[:3]:
         load.wait()
-    gather_round(0, 0, 0)
-    gather_round(1, 0, 0)
+    rounds(0, 0)
     load_x.wait()
-    lax.fori_loop(0, 8, lambda i, _: (norm_rows(i, xs), 0)[1], 0)
-    gather_round(0, 0, 1)
-    gather_round(1, 0, 1)
+    loop(0, 8, lambda i: norm_rows(i, xs))
+    rounds(0, 1)
     load_dy.wait()
-    lax.fori_loop(0, 8, lambda i, _: (transpose_rows(i, do, dot_do), 0)[1], 0)
-    for r in (2, 3, 4):
-        gather_round(0, 0, r)
-        gather_round(1, 0, r)
+    loop(0, 3, lambda i: transpose_rows(i, do, dot_do))
+    rounds(0, 2)
+    loop(3, 6, lambda i: transpose_rows(i, do, dot_do))
+    rounds(0, 3)
     for load in loads[3:]:
         load.wait()
-    gather_round(0, 1, 0)
-    gather_round(1, 1, 0)
-    gather_round(0, 0, 5)
+    rounds(1, 0)
+    loop(6, 8, lambda i: transpose_rows(i, do, dot_do))
+    rounds(0, 4)
+    rounds(0, 5)
     gathered(0, 0)
-    gather_round(1, 0, 5)
-
-    def hidden(i, _):
+    gathered(1, 0)
+
+    later = [(kind, r) for r in range(1, 6) for kind in range(3)]
+    slots = [4 * (r - 1) + kind + 1 for kind, r in later]
+
+    def between(i, first, end):
+        for slot, (kind, r) in zip(slots, later, strict=True):
+            if first <= slot < end:
+
+                @pl.when(i == slot)
+                def _(kind=kind, r=r):
+                    gather_round(kind, 1, r)
+
+    def hidden(i):
+        rows = span(lax.div(i, 2) * tm, tm)
+        here = a[rows, :]
+        for c in range(CHUNKS // 2):
+            cols = span((lax.rem(i, 2) * (CHUNKS // 2) + c) * fc, fc)
+            gate, up = dot(here, wgu[0, 0, :, cols]), dot(here, wgu[0, 1, :, cols])
+            by_gu[0, rows, cols] = (gate * sigmoid(gate) * up).astype(BF16)
+        between(i, 0, 16)
+
+    loop(0, 16, hidden)
+    gathered(2, 0)
+
+    def down(i):
         rows = span(i * tm, tm)
-        here = a[rows, :]
-        for c in range(CHUNKS):
-            cols = slice(c * fc, (c + 1) * fc)
-            gate, up = dot(here, wgu[0, 0, :, cols]), dot(here, wgu[0, 1, :, cols])
-            big[rows, cols] = (gate * sigmoid(gate) * up).astype(BF16)
-        return 0
-
-    lax.fori_loop(0, 2, hidden, 0)
-    gather_round(0, 1, 1)
-    gather_round(1, 1, 1)
-    lax.fori_loop(2, 4, hidden, 0)
-    gather_round(0, 1, 2)
-    gather_round(1, 1, 2)
-    lax.fori_loop(4, 6, hidden, 0)
-    gather_round(0, 1, 3)
-    gather_round(1, 1, 3)
-    lax.fori_loop(6, 8, hidden, 0)
-    gathered(1, 0)
-
-    def down(i, _):
-        rows = span(i * tm, tm)
-        h = (xs[rows, :].astype(F32) + dot(big[rows, :], wd[0]).astype(BF16).astype(F32)).astype(BF16)
+        h = (xs[rows, :].astype(F32) + dot(by_gu[0, rows, :], wd[0]).astype(BF16).astype(F32)).astype(BF16)
         h1[rows, :] = h
         wide = h.astype(F32)
-        normed = wide * scale_of(wide)
-        a[rows, :] = normed.astype(BF16)
-        at[:, rows] = normed.astype(BF16).astype(F32).T.astype(BF16)
-        return 0
-
-    lax.fori_loop(0, 3, down, 0)
-    gather_round(0, 1, 4)
-    gather_round(1, 1, 4)
-    lax.fori_loop(3, 8, down, 0)
-    gather_round(0, 1, 5)
-    gather_round(1, 1, 5)
-    gathered(0, 1)
-    gathered(1, 1)
-
-    act_cols, gate_cols, up_cols = (slice(k * fc, (k + 1) * fc) for k in range(3))
+        normed = (wide * scale_of(wide)).astype(BF16)
+        a[rows, :] = normed
+        at[:, rows] = normed.astype(F32).T.astype(BF16)
+        between(i + 16, 16, 24)
+
+    loop(0, 8, down)
+    for kind in range(3):
+        gathered(kind, 1)
 
     for lam in range(2):
         number = 1 - lam
 
-        def quarter(c, _, lam=lam, number=number):
+        def quarter(c, lam=lam, number=number):
             cols = span(c * fc, fc)
-            t0 = (lam * CHUNKS + c) * PHASE
-
-            def rows_of(i, _):
+            t0 = lam * PERIOD + c * PHASE
+
+            def rows_of(i):
                 rows = span(i * tb, tb)
                 here = a[rows, :]
                 gate, up = dot(here, wgu[number, 0, :, cols]), dot(here, wgu[number, 1, :, cols])
                 by_act = dot_t(do[rows, :], wd[number, cols, :]).astype(BF16).astype(F32)
                 sig = sigmoid(gate)
                 silu = gate * sig
-                big[rows, act_cols] = (silu * up).astype(BF16)
-                big[rows, up_cols] = (by_act * silu).astype(BF16)
-                big[rows, gate_cols] = (by_act * up * (sig + silu * (1.0 - sig))).astype(BF16)
+                act[rows, :] = (silu * up).astype(BF16)
+                by_gu[1, rows, cols] = (by_act * silu).astype(BF16)
+                by_gu[0, rows, cols] = (by_act * up * (sig + silu * (1.0 - sig))).astype(BF16)
                 tick(t0 + i)
-                return 0
-
-            lax.fori_loop(0, 4, rows_of, 0)
-            gu[lam, 0, :, cols] = dot(at[...], big[:, gate_cols]).astype(BF16)
+
+            loop(0, 4, rows_of)
+            gu[lam, 0, :, cols] = dot(at[...], by_gu[0, :, cols]).astype(BF16)
             tick(t0 + 4)
-            gu[lam, 1, :, cols] = dot(at[...], big[:, up_cols]).astype(BF16)
+            gu[lam, 1, :, cols] = dot(at[...], by_gu[1, :, cols]).astype(BF16)
             tick(t0 + 5)
-            gd[lam, :, cols] = dot(dot_do[...], big[:, act_cols]).astype(BF16)
-            tick(t0 + 6)
-            if lam == 0:
-
-                def by_input(i, _):
-                    rows = span(i * tb, tb)
-                    by_a = dot_t(big[rows, gate_cols], wgu[number, 0, :, cols]) + dot_t(big[rows, up_cols], wgu[number, 1, :, cols])
-
-                    @pl.when(c == 0)
-                    def _():
-                        acc[rows, :] = by_a
-
-                    @pl.when(c > 0)
-                    def _():
-                        acc[rows, :] += by_a
-
-                    return 0
-
-                lax.fori_loop(0, 4, by_input, 0)
-            tick(t0 + 7)
-            return 0
-
-        lax.fori_loop(0, CHUNKS, quarter, 0)
+
+            def by_down(i):
+                rows = span(i * rows_d, rows_d)
+                gd[lam, rows, cols] = dot(dot_do[rows, :], act[...]).astype(BF16)
+                tick(t0 + 6 + i)
+
+            loop(0, 2, by_down)
+
+        loop(0, CHUNKS, quarter)
 
         if lam == 0:
-
-            def through_norm(i, _):
+            t0 = CHUNKS * PHASE
+
+            def by_input(i, number=number, t0=t0):
                 rows = span(i * tm, tm)
-                by_a = acc[rows, :].astype(BF16).astype(F32)
+                by_a = dot_t(by_gu[0, rows, :], wgu[number, 0]) + dot_t(by_gu[1, rows, :], wgu[number, 1])
+                by_a = by_a.astype(BF16).astype(F32)
                 wide = h1[rows, :].astype(F32)
                 scale = scale_of(wide)
                 inner = jnp.mean(by_a * wide, -1, keepdims=True)
@@ -401,17 +394,18 @@
                 normed = (wide * scale_of(wide)).astype(BF16)
                 a[rows, :] = normed
                 at[:, rows] = normed.astype(F32).T.astype(BF16)
-                return 0
-
-            lax.fori_loop(0, 8, through_norm, 0)
-
-    last = 2 * CHUNKS * PHASE + 4 * SPACING + 3
-    lax.fori_loop(2 * CHUNKS * PHASE, last, lambda t, _: (tick(t), 0)[1], 0)
+                tick(t0 + i)
+
+            loop(0, 8, by_input)
+
+    loop(PERIOD + CHUNKS * PHASE, PERIOD + CHUNKS * PHASE + 4 * SPACING + 2, tick)
 
     outs = []
     for lam in range(2):
-        outs.append(pltpu.make_async_copy(gu.at[lam, :, span(me * own_d, own_d), :], gu_out.at[1 - lam], out_sem.at[lam, 0]))
-        outs.append(pltpu.make_async_copy(gd.at[lam, :, span(me * own_f, own_f)], gd_out.at[1 - lam], out_sem.at[lam, 1]))
+        for kind, out in enumerate((g_out, u_out)):
+            own = gu.at[lam, kind, span(me * own_d, own_d), :]
+            outs.append(pltpu.make_async_copy(own, out.at[1 - lam], out_sem.at[lam, kind]))
+        outs.append(pltpu.make_async_copy(d_own.at[lam], d_out.at[1 - lam], out_sem.at[lam, 2]))
     for out in outs:
         out.start()
     lanes = all_squares.shape[2]
@@ -434,9 +428,9 @@
     for copy in copies:
         copy.wait()
     total = jnp.sum(all_squares[...])
-    count = n * (gu_out.size + gd_out.size)
+    count = n * (g_out.size + u_out.size + d_out.size)
     factor_out[...] = jnp.minimum(1.0, 0.5 * lax.rsqrt(jnp.full(factor_out.shape, total, F32) / count + 1e-30))
-    for kind in range(2):
+    for kind in range(3):
         for number in range(2):
             await_eighths(kind, number, 56, ag_send.at[kind, number])
     for out in outs:
@@ -448,6 +442,15 @@
     v = 0.95 * v + 0.05 * g * g
     step = m * lax.rsqrt(v + 1e-8) + 0.1 * w
     return (w - 0.02 * step).astype(jnp.bfloat16), m, v
+
+
+def update(factor, *refs):
+    ins, outs = refs[:12], refs[12:]
+    for i in range(3):
+        w, m, v, g = (ins[3 * k + i] for k in range(4))
+        new = adamw(w[...].astype(F32), m[...], v[...], g[...].astype(F32) * factor[0, 0])
+        for k in range(3):
+            outs[3 * k + i][...] = new[k]
 
 
 def solution(mesh):
@@ -462,39 +465,41 @@
         fc = ff // CHUNKS
         lanes = min(128, own_f)
         anywhere = pl.BlockSpec(memory_space=pl.ANY)
-        grads_gu, grads_gd, factor = pl.pallas_call(
+        *gradients, factor = pl.pallas_call(
             functools.partial(kernel, n, across),
             out_shape=(
-                jax.ShapeDtypeStruct((layers, 2, own_d, ff), BF16),
-                jax.ShapeDtypeStruct((layers, d, own_f), BF16),
+                jax.ShapeDtypeStruct((layers, own_d, ff), BF16),
+                jax.ShapeDtypeStruct((layers, own_d, ff), BF16),
+                jax.ShapeDtypeStruct((layers, own_f, d), BF16),
                 jax.ShapeDtypeStruct((8, lanes), F32),
             ),
             in_specs=[anywhere] * 5,
-            out_specs=(anywhere, anywhere, pl.BlockSpec(memory_space=pltpu.VMEM)),
+            out_specs=(anywhere, anywhere, anywhere, pl.BlockSpec(memory_space=pltpu.VMEM)),
             scratch_shapes=[
                 pltpu.VMEM((layers, 2, d, ff), BF16),
                 pltpu.VMEM((layers, ff, d), BF16),
                 pltpu.VMEM((layers, 2, d, ff), BF16),
                 pltpu.VMEM((layers, d, ff), BF16),
-                pltpu.VMEM((CHUNKS, 2, 4, 2, own_d, fc), BF16),
-                pltpu.VMEM((2, 2, 4, d // 2, own_f), BF16),
+                pltpu.VMEM((CHUNKS, 2, 2, 7 * own_d // 2, fc), BF16),
+                pltpu.VMEM((2, 2, 7 * d // 4, own_f), BF16),
                 pltpu.VMEM((tokens, d), BF16),
                 pltpu.VMEM((tokens, d), BF16),
                 pltpu.VMEM((tokens, d), BF16),
                 pltpu.VMEM((tokens, d), BF16),
                 pltpu.VMEM((d, tokens), BF16),
                 pltpu.VMEM((d, tokens), BF16),
-                pltpu.VMEM((tokens, ff), BF16),
-                pltpu.VMEM((tokens, d), F32),
+                pltpu.VMEM((tokens, fc), BF16),
+                pltpu.VMEM((2, tokens, ff), BF16),
+                pltpu.VMEM((layers, own_f, d), BF16),
                 pltpu.VMEM((8, fc), F32),
                 pltpu.VMEM((8, own_f), F32),
                 pltpu.VMEM((n, 8, lanes), F32),
                 pltpu.SemaphoreType.DMA((2, 4)),
-                pltpu.SemaphoreType.DMA((2, 2)),
-                pltpu.SemaphoreType.DMA((2, 2)),
-                pltpu.SemaphoreType.DMA((2, 2, 4)),
-                pltpu.SemaphoreType.DMA((2, 2, 4)),
-                pltpu.SemaphoreType.DMA((2, 2)),
+                pltpu.SemaphoreType.DMA((2, 3)),
+                pltpu.SemaphoreType.DMA((3, 2)),
+                pltpu.SemaphoreType.DMA((3, 2, 4)),
+                pltpu.SemaphoreType.DMA((3, 2, 4)),
+                pltpu.SemaphoreType.DMA((3, 2)),
                 pltpu.SemaphoreType.DMA((CHUNKS + 2, 2)),
                 pltpu.SemaphoreType.DMA((CHUNKS + 2, 2, 4)),
                 pltpu.SemaphoreType.DMA((n - 1,)),
@@ -503,10 +508,23 @@
             compiler_params=pltpu.CompilerParams(collective_id=0, has_side_effects=True, vmem_limit_bytes=67043328),
             name="train_step",
         )(x, dy, *weights)
-        factor = factor[0, 0]
-        gradients = [grads_gu[:, 0], grads_gu[:, 1], jnp.swapaxes(grads_gd, 1, 2)]
-        new = [adamw(w.astype(F32), m, v, g.astype(F32) * factor) for w, m, v, g in zip(weights, m, v, gradients, strict=True)]
-        return tuple(one[which] for which in range(3) for one in new)
+        pieces = 4
+
+        def blocks(arrays):
+            return tuple(
+                pl.BlockSpec((1, one.shape[1] // pieces, one.shape[2]), lambda layer, piece: (layer, piece, 0)) for one in arrays
+            )
+
+        shapes = [jax.ShapeDtypeStruct(one.shape, kind) for kind in (BF16, F32, F32) for one in weights]
+        inputs = (*weights, *m, *v, *gradients)
+        return pl.pallas_call(
+            update,
+            grid=(layers, pieces),
+            out_shape=tuple(shapes),
+            in_specs=[pl.BlockSpec(memory_space=pltpu.SMEM), *blocks(inputs)],
+            out_specs=blocks(shapes),
+            name="adamw",
+        )(factor, *inputs)
 
     states, cut = P(("rep", "dp"), None, None), P(None, "dp", None)
     return jax.shard_map(

time: 243 us -> 213 us (0.88)
  Pallas kernels: 224 us -> 212 us
  other arithmetic: 10.1 us -> 0 us
  local copies, waits for them, and re-layouts: 8.68 us -> 0 us
    pallas_call x1, Pallas kernels: 224 us -> 203 us  [step(): pl.pallas_call(functools.partial(kernel, n, across), out_shape=(jax.Shape...]
    convert_element_type x2 -> x0, other arithmetic: 10.1 us -> none  [adamw(): return ((w - 0.02 * step).astype(jnp.bfloat16), m, v)]
    pallas_call x0 -> x1, Pallas kernels: none -> 9.19 us  [step(): pl.pallas_call(update, grid=(layers, pieces), out_shape=tuple(shapes), in...]
    unnamed x12 -> x0, local copies, waits for them, and re-layouts: 7.49 us -> none
where the time goes in v2:
time: 213 us
  Pallas kernels  212 us (100%)
    pallas_call x1, Pallas kernels, step(): pl.pallas_call(functools.partial(kernel, n, across), out_shape=(jax.Shape...  203 us
    pallas_call x1, Pallas kernels, step(): pl.pallas_call(update, grid=(layers, pieces), out_shape=tuple(shapes), in...  9.19 us

profile of v2, /device:TPU:22, one launch (start us, length us, event | category | flops | bytes accessed | tf_op | source)
XLA Modules:
  0.0 212.8 jit_solution(454236750475771701)
XLA Ops:
  0.6 202.8 %train_step.1 = (bf16[2,64,2048]{2,1,0:T(8,128)(2,1)}, bf16[2,64,2048]{2,1,0:T(8,128)(2,1)}, bf16[2,256,512]{2,1,0:T(8,128)(2,1)}, f32[8,128]{1,0:T(8,128)}) custom-call(bf16[1,2048,512]{2,1,0:T(8,128)(2,1)} %x_in.1, bf16[1,2048,512]{2,1,0:T(8,128)(2,1)} %dy_in.1, bf16[2,64,2048]{2,1,0:T(8,128)(2,1)} %refs_0_.1, bf16[2,64,2048]{2,1,0:T(8,128)(2,1)} %refs_1_.1, ...), custom_call_target="tpu_custom_call" | custom-call | tf_op jit(solution)/shard_map/train_step/pallas_call | solution.py:468
  203.5 9.2 %adamw.1 = (bf16[2,64,2048]{2,1,0:T(8,128)(2,1)}, bf16[2,64,2048]{2,1,0:T(8,128)(2,1)}, bf16[2,256,512]{2,1,0:T(8,128)(2,1)}, f32[2,64,2048]{2,1,0:T(8,128)}, f3...) custom-call(f32[8,128]{1,0:T(8,128)} %get-tuple-element.13.factor, ...), custom_call_target="tpu_custom_call" | custom-call | tf_op jit(solution)/shard_map/adamw/pallas_call | solution.py:520

commit v3 on v2

--- a/solution.py
+++ b/solution.py
@@ -110,18 +110,19 @@
         load.start()
     pl.semaphore_wait(barrier, len(partners))
 
-    eighth_f, eighth_r = ff // 8, own_f // 8
+    eighth_f, eighth_r = ff // 16, own_f // 8
     mine = 4 * core + 2 * parity
     theirs = 4 * core + 2 * (1 - parity)
 
     def part(kind, number, shard, eighth, count):
-        if kind < 2:
-            return wgu.at[number, kind, span(shard * own_d, own_d), pl.ds(pl.multiple_of(eighth * eighth_f, eighth_f), count * eighth_f)]
+        if kind < 4:
+            column = pl.multiple_of((kind // 2 * 8 + eighth) * eighth_f, eighth_f)
+            return wgu.at[number, kind % 2, span(shard * own_d, own_d), pl.ds(column, count * eighth_f)]
         return wd.at[number, pl.ds(pl.multiple_of(shard * own_f + eighth * eighth_r, eighth_r), count * eighth_r), :]
 
     def bytes_of(kind, number, eighths):
-        if kind < 2:
-            return wgu.at[number, kind, pl.ds(0, eighths * own_d // 8), :]
+        if kind < 4:
+            return wgu.at[number, kind % 2, pl.ds(0, eighths * own_d // 8), pl.ds(0, ff // 2)]
         return wd.at[number, pl.ds(0, eighths * eighth_r), :]
 
     def await_eighths(kind, number, eighths, sem):
@@ -267,7 +268,6 @@
     squares_gu[...] = jnp.zeros_like(squares_gu)
     squares_gd[...] = jnp.zeros_like(squares_gd)
     tm = tokens // 8
-    tb = tokens // 4
 
     def norm_rows(i, src):
         rows = span(i * tm, tm)
@@ -278,68 +278,79 @@
         rows = span(i * tm, tm)
         dst[:, rows] = src[rows, :].astype(F32).T.astype(BF16)
 
-    def rounds(number, r, kinds=(0, 1, 2)):
-        for kind in kinds:
-            gather_round(kind, number, r)
-
     def loop(first, end, body):
         lax.fori_loop(first, end, lambda i, _: (body(i), 0)[1], 0)
 
+    first, second, third = "1024..3.1..0.2.56310243106298.1036415029837", "....5.46..239.5.476...594..6..5.9.....9..7", "..8..7...8..7.8.....78."
+    early, woven, taken, slot = [], [], [0] * 10, -1
+    for place, mark in enumerate(first + second + third):
+        if mark == ".":
+            slot += place >= len(first)
+            early += [None] * (place < len(first))
+        else:
+            number, kind = divmod(int(mark), 5)
+            one = (number, kind, taken[int(mark)])
+            taken[int(mark)] += 1
+            (woven if place >= len(first) else early).append((slot, *one) if place >= len(first) else one)
+
+    def between(i, *ranges):
+        for slot, number, kind, r in woven:
+            if any(slot in one for one in ranges):
+
+                @pl.when(i == slot)
+                def _(number=number, kind=kind, r=r):
+                    gather_round(kind, number, r)
+
     for load in loads[:3]:
         load.wait()
-    rounds(0, 0)
-    load_x.wait()
-    loop(0, 8, lambda i: norm_rows(i, xs))
-    rounds(0, 1)
-    load_dy.wait()
-    loop(0, 3, lambda i: transpose_rows(i, do, dot_do))
-    rounds(0, 2)
-    loop(3, 6, lambda i: transpose_rows(i, do, dot_do))
-    rounds(0, 3)
-    for load in loads[3:]:
-        load.wait()
-    rounds(1, 0)
-    loop(6, 8, lambda i: transpose_rows(i, do, dot_do))
-    rounds(0, 4)
-    rounds(0, 5)
-    gathered(0, 0)
-    gathered(1, 0)
-
-    later = [(kind, r) for r in range(1, 6) for kind in range(3)]
-    slots = [4 * (r - 1) + kind + 1 for kind, r in later]
-
-    def between(i, first, end):
-        for slot, (kind, r) in zip(slots, later, strict=True):
-            if first <= slot < end:
-
-                @pl.when(i == slot)
-                def _(kind=kind, r=r):
-                    gather_round(kind, 1, r)
+    waiting = [
+        lambda: (load_x.wait(), loop(0, 4, lambda i: norm_rows(i, xs))),
+        lambda: loop(4, 8, lambda i: norm_rows(i, xs)),
+        lambda: [load.wait() for load in loads[3:]],
+        lambda: (load_dy.wait(), loop(0, 2, lambda i: transpose_rows(i, do, dot_do))),
+        lambda: loop(2, 4, lambda i: transpose_rows(i, do, dot_do)),
+        lambda: loop(4, 6, lambda i: transpose_rows(i, do, dot_do)),
+        lambda: loop(6, 8, lambda i: transpose_rows(i, do, dot_do)),
+    ]
+    for one in early:
+        if one:
+            number, kind, r = one
+            gather_round(kind, number, r)
+        else:
+            waiting.pop(0)() if waiting else None
+    for kind in range(2):
+        gathered(kind, 0)
 
     def hidden(i):
-        rows = span(lax.div(i, 2) * tm, tm)
+        rows = span(lax.rem(i, 8) * tm, tm)
         here = a[rows, :]
-        for c in range(CHUNKS // 2):
-            cols = span((lax.rem(i, 2) * (CHUNKS // 2) + c) * fc, fc)
-            gate, up = dot(here, wgu[0, 0, :, cols]), dot(here, wgu[0, 1, :, cols])
+        parts = [span((lax.div(i, 8) * (CHUNKS // 2) + c) * fc, fc) for c in range(CHUNKS // 2)]
+        products = [(dot(here, wgu[0, 0, :, cols]), dot(here, wgu[0, 1, :, cols])) for cols in parts]
+        for cols, (gate, up) in zip(parts, products, strict=True):
             by_gu[0, rows, cols] = (gate * sigmoid(gate) * up).astype(BF16)
-        between(i, 0, 16)
-
-    loop(0, 16, hidden)
-    gathered(2, 0)
+        between(i, range(16))
+
+    loop(0, 8, hidden)
+    for kind in (2, 3):
+        gathered(kind, 0)
+    loop(8, 16, hidden)
+    gathered(4, 0)
 
     def down(i):
-        rows = span(i * tm, tm)
-        h = (xs[rows, :].astype(F32) + dot(by_gu[0, rows, :], wd[0]).astype(BF16).astype(F32)).astype(BF16)
-        h1[rows, :] = h
-        wide = h.astype(F32)
-        normed = (wide * scale_of(wide)).astype(BF16)
-        a[rows, :] = normed
-        at[:, rows] = normed.astype(F32).T.astype(BF16)
-        between(i + 16, 16, 24)
-
-    loop(0, 8, down)
-    for kind in range(3):
+        both = [span((2 * i + k) * tm, tm) for k in range(2)]
+        products = [dot(by_gu[0, rows, :], wd[0]) for rows in both]
+        for rows, product in zip(both, products, strict=True):
+            h = (xs[rows, :].astype(F32) + product.astype(BF16).astype(F32)).astype(BF16)
+            h1[rows, :] = h
+            wide = h.astype(F32)
+            normed = (wide * scale_of(wide)).astype(BF16)
+            a[rows, :] = normed
+            at[:, rows] = normed.astype(F32).T.astype(BF16)
+        between(2 * i + 16, (16, 18, 20, 22))
+        between(2 * i + 17, (17, 19, 21, 23))
+
+    loop(0, 4, down)
+    for kind in (0, 1, 4):
         gathered(kind, 1)
 
     for lam in range(2):
@@ -348,18 +359,29 @@
         def quarter(c, lam=lam, number=number):
             cols = span(c * fc, fc)
             t0 = lam * PERIOD + c * PHASE
+            if lam == 0:
+
+                @pl.when(c == CHUNKS // 2)
+                def _():
+                    for kind in (2, 3):
+                        gathered(kind, 1)
 
             def rows_of(i):
-                rows = span(i * tb, tb)
-                here = a[rows, :]
-                gate, up = dot(here, wgu[number, 0, :, cols]), dot(here, wgu[number, 1, :, cols])
-                by_act = dot_t(do[rows, :], wd[number, cols, :]).astype(BF16).astype(F32)
-                sig = sigmoid(gate)
-                silu = gate * sig
-                act[rows, :] = (silu * up).astype(BF16)
-                by_gu[1, rows, cols] = (by_act * silu).astype(BF16)
-                by_gu[0, rows, cols] = (by_act * up * (sig + silu * (1.0 - sig))).astype(BF16)
+                both = [span((2 * i + k) * tm, tm) for k in range(2)]
+                products = [
+                    (dot(a[rows, :], wgu[number, 0, :, cols]), dot(a[rows, :], wgu[number, 1, :, cols]), dot_t(do[rows, :], wd[number, cols, :]))
+                    for rows in both
+                ]
+                for rows, (gate, up, by_act) in zip(both, products, strict=True):
+                    by_act = by_act.astype(BF16).astype(F32)
+                    sig = sigmoid(gate)
+                    silu = gate * sig
+                    act[rows, :] = (silu * up).astype(BF16)
+                    by_gu[1, rows, cols] = (by_act * silu).astype(BF16)
+                    by_gu[0, rows, cols] = (by_act * up * (sig + silu * (1.0 - sig))).astype(BF16)
                 tick(t0 + i)
+                if lam == 0:
+                    between(t0 + i + 24, range(24, 28), range(32, 36))
 
             loop(0, 4, rows_of)
             gu[lam, 0, :, cols] = dot(at[...], by_gu[0, :, cols]).astype(BF16)
@@ -371,6 +393,8 @@
                 rows = span(i * rows_d, rows_d)
                 gd[lam, rows, cols] = dot(dot_do[rows, :], act[...]).astype(BF16)
                 tick(t0 + 6 + i)
+                if lam == 0:
+                    between(t0 + i + 30, range(30, 32), range(38, 40))
 
             loop(0, 2, by_down)
 
@@ -430,7 +454,7 @@
     total = jnp.sum(all_squares[...])
     count = n * (g_out.size + u_out.size + d_out.size)
     factor_out[...] = jnp.minimum(1.0, 0.5 * lax.rsqrt(jnp.full(factor_out.shape, total, F32) / count + 1e-30))
-    for kind in range(3):
+    for kind in range(5):
         for number in range(2):
             await_eighths(kind, number, 56, ag_send.at[kind, number])
     for out in outs:
@@ -496,10 +520,10 @@
                 pltpu.VMEM((n, 8, lanes), F32),
                 pltpu.SemaphoreType.DMA((2, 4)),
                 pltpu.SemaphoreType.DMA((2, 3)),
-                pltpu.SemaphoreType.DMA((3, 2)),
-                pltpu.SemaphoreType.DMA((3, 2, 4)),
-                pltpu.SemaphoreType.DMA((3, 2, 4)),
-                pltpu.SemaphoreType.DMA((3, 2)),
+                pltpu.SemaphoreType.DMA((5, 2)),
+                pltpu.SemaphoreType.DMA((5, 2, 4)),
+                pltpu.SemaphoreType.DMA((5, 2, 4)),
+                pltpu.SemaphoreType.DMA((5, 2)),
                 pltpu.SemaphoreType.DMA((CHUNKS + 2, 2)),
                 pltpu.SemaphoreType.DMA((CHUNKS + 2, 2, 4)),
                 pltpu.SemaphoreType.DMA((n - 1,)),
@@ -508,7 +532,7 @@
             compiler_params=pltpu.CompilerParams(collective_id=0, has_side_effects=True, vmem_limit_bytes=67043328),
             name="train_step",
         )(x, dy, *weights)
-        pieces = 4
+        pieces = 2
 
         def blocks(arrays):
             return tuple(

time: 213 us -> 207 us (0.972)
  Pallas kernels: 212 us -> 206 us
    pallas_call x1, Pallas kernels: 203 us -> 199 us  [step(): pl.pallas_call(functools.partial(kernel, n, across), out_shape=(jax.Shape...]
where the time goes in v3:
time: 207 us
  Pallas kernels  206 us (100%)
    pallas_call x1, Pallas kernels, step(): pl.pallas_call(functools.partial(kernel, n, across), out_shape=(jax.Shape...  199 us
    pallas_call x1, Pallas kernels, step(): pl.pallas_call(update, grid=(layers, pieces), out_shape=tuple(shapes), in...  7.31 us

profile of v3, /device:TPU:22, one launch (start us, length us, event | category | flops | bytes accessed | tf_op | source)
XLA Modules:
  0.0 206.7 jit_solution(13105868722470951898)
XLA Ops:
  0.6 198.6 %train_step.1 = (bf16[2,64,2048]{2,1,0:T(8,128)(2,1)}, bf16[2,64,2048]{2,1,0:T(8,128)(2,1)}, bf16[2,256,512]{2,1,0:T(8,128)(2,1)}, f32[8,128]{1,0:T(8,128)}) custom-call(bf16[1,2048,512]{2,1,0:T(8,128)(2,1)} %x_in.1, bf16[1,2048,512]{2,1,0:T(8,128)(2,1)} %dy_in.1, bf16[2,64,2048]{2,1,0:T(8,128)(2,1)} %refs_0_.1, bf16[2,64,2048]{2,1,0:T(8,128)(2,1)} %refs_1_.1, ...), custom_call_target="tpu_custom_call" | custom-call | tf_op jit(solution)/shard_map/train_step/pallas_call | solution.py:492
  199.2 7.3 %adamw.1 = (bf16[2,64,2048]{2,1,0:T(8,128)(2,1)}, bf16[2,64,2048]{2,1,0:T(8,128)(2,1)}, bf16[2,256,512]{2,1,0:T(8,128)(2,1)}, f32[2,64,2048]{2,1,0:T(8,128)}, f3...) custom-call(f32[8,128]{1,0:T(8,128)} %get-tuple-element.13.factor, ...), custom_call_target="tpu_custom_call" | custom-call | tf_op jit(solution)/shard_map/adamw/pallas_call | solution.py:544
